TPU v7x, 16 devices: a 4x2x1 block of a 4x4x8 slice. The times are simulated.
16 devices in a mesh: ens: 2 (over y, z), feat: 8 (over x, core).
Axes of the slice: x: 4, y: 2, z: 1, core: 2. Of those that a mesh axis runs over, the one named last changes fastest.
The devices are a block of a 4x4x8 slice.
Arguments:
- particles: float32 [4, 512, 16384], P('ens', None, 'feat'), parts along dimension 0
- target_mean: float32 [4, 16384], P('ens', 'feat'), parts along dimension 0
- precision: float32 [32768], P(('ens', 'feat')), parts along dimension 0
- low_factor: bfloat16 [32768, 64], P(('ens', 'feat')), parts along dimension 0
Outputs:
- output: float32 [4, 512, 16384], P('ens', None, 'feat'), parts along dimension 0
There are 2 independent parts. A program takes and returns all parts, laid end to end along the dimension named above; each array names one.
All inputs are finite; a program needn't handle non-finite values.
Results may differ from a plain program's by a relative error of at most 0.001.
Values are sent between devices in bfloat16 or wider.
A program may use at most 768 MiB of HBM per device.

v0:
```python
import jax
import jax.numpy as jnp
from jax import lax
from jax.sharding import PartitionSpec as P

NUM_STEPS = 3


def solution(mesh):
    feat_count = mesh.shape["feat"]
    data_spec = P("ens", None, "feat")
    mean_spec = P("ens", "feat")
    prec_spec = P(("ens", "feat"))
    factor_spec = P(("ens", "feat"), None)

    def local_steps(particles, target_mean, precision, low_factor):
        num_part = particles.shape[1]
        total_feat = particles.shape[2] * feat_count
        bandwidth = 2.0 * total_feat
        step_size = 0.25 * total_feat
        mean_rows = target_mean[:, None, :]
        theta = particles
        for step_index in range(NUM_STEPS):
            centered = theta - mean_rows
            theta_bf = theta.astype(jnp.bfloat16)
            proj_part = jnp.einsum("end,dr->enr", centered.astype(jnp.bfloat16), low_factor, preferred_element_type=jnp.float32)
            gram_part = jnp.einsum("end,emd->enm", theta_bf, theta_bf, preferred_element_type=jnp.float32)
            project, gram_mat = lax.psum((proj_part, gram_part), "feat")
            gram_diag = jnp.diagonal(gram_mat, axis1=1, axis2=2)
            sq_dist = jnp.maximum(gram_diag[:, :, None] + gram_diag[:, None, :] - 2.0 * gram_mat, 0.0)
            kernel = jnp.exp(-sq_dist / bandwidth)
            low_term = jnp.einsum("enr,dr->end", project.astype(jnp.bfloat16), low_factor, preferred_element_type=jnp.float32)
            grad_log = -(centered * precision + low_term)
            mixed = (grad_log - (2.0 / bandwidth) * theta).astype(jnp.bfloat16)
            drive = jnp.einsum("enm,emd->end", kernel.astype(jnp.bfloat16), mixed, preferred_element_type=jnp.float32)
            row_sum = jnp.sum(kernel, axis=2, keepdims=True)
            theta = theta + step_size * ((drive + (2.0 / bandwidth) * row_sum * theta) / num_part)
        return theta

    return jax.shard_map(local_steps, mesh=mesh, in_specs=(data_spec, mean_spec, prec_spec, factor_spec), out_specs=data_spec, check_vma=False)
```

profile of v0, /device:TPU:113, one launch (start us, length us, event | category | flops | bytes accessed | tf_op | source)
XLA Modules:
  0.0 459.2 jit_solution(7641933153848074394)
XLA Ops:
  6.6 9.5 %fusion.10 = f32[2,512,512]{2,1,0:T(8,128)} fusion(f32[2,512,2048]{2,1,0:T(8,128)} %param.4), kind=kOutput, calls=%fused_computation.22 | convolution fusion | flops 2149580800 | bytes 10485760 | tf_op jit(solution)/shard_map/end,emd->enm/dot_general | solution.py:27
  16.2 4.6 %fusion = f32[2,512,64]{2,1,0:T(8,128)S(1)} fusion(f32[2,512,2048]{2,1,0:T(8,128)} %param.4, f32[2,2048]{1,0:T(2,128)S(1)} %copy-done.4, bf16[2048,64]{0,1:T(8,128)(2,1)S(1)} %copy-done), kind=kOutput, calls=%fused_computation.12 | convolution fusion | flops 272629760 | bytes 8929280 | tf_op jit(solution)/shard_map/end,dr->enr/dot_general | solution.py:26
  20.8 31.3 %all-reduce.12 = bf16[2,512,64]{2,1,0:T(8,128)(2,1)S(1)} all-reduce(f32[2,512,64]{2,1,0:T(8,128)S(1)} %fusion), channel_id=1, replica_groups=mesh['ens'=2,'feat'=8] {'feat'}, use_global_device_ids=true, to_apply=%region_1.0 | all-reduce | flops 65536 | bytes 393216 | tf_op jit(solution)/shard_map/psum | solution.py:28
  52.1 24.6 %all-reduce.7.cloned.1.call-done = f32[2,512,512]{2,1,0:T(8,128)} async-done(((f32[2,512,512]{2,1,0:T(8,128)}), f32[2,512,512]{2,1,0:T(8,128)}) %all-reduce.7.cloned.1.call-update) | async-done | bytes 2097168 | tf_op jit(solution)/shard_map/psum | solution.py:28
  76.7 60.2 %copy.14 = f32[2,512,512]{0,2,1:T(8,128)} copy(f32[2,512,512]{2,1,0:T(8,128)} %all-reduce.7.cloned.1.call-done) | data formatting | bytes 4194304 | tf_op jit(solution)/shard_map/psum | solution.py:28
  137.0 5.5 %gather_fusion = f32[512,2]{1,0:T(8,128)S(1)} fusion(f32[2,512,512]{0,2,1:T(8,128)} %copy.14, s32[512]{0:T(512)S(1)} %bitcast.23), kind=kCustom, calls=%fused_computation | custom fusion | bytes 12288 | tf_op jit(solution)/shard_map/jit(diagonal)/gather | solution.py:29
  142.6 0.8 fusion.12
  143.4 13.0 %multiply_add_fusion.2 = f32[2,512,2048]{2,1,0:T(8,128)} fusion(f32[2,512,2048]{2,1,0:T(8,128)} %param.4, f32[2,512]{1,0:T(2,128)S(1)} %broadcast_multiply_fusion.2, f32[2048]{0:T(1024)S(1)} %copy-done.5, f32[2,2048]{1,0:T(2,128)S(1)} %copy-done.4, f32[2,512,512]{2,1,0:T(8,128)S(1)} %copy-done.1, f32[2,512]{1,0:T(2,128)S(1)} %copy.15, ...), kind=kOutput, calls=%fused_computation.7 | convolution fusion | flops 2442657792 | bytes 19300352 | tf_op jit(solution)/shard_map/enm,emd->end/dot_general | solution.py:35
  156.4 9.5 %fusion.5 = f32[2,512,512]{2,1,0:T(8,128)} fusion(f32[2,512,2048]{2,1,0:T(8,128)} %multiply_add_fusion.2), kind=kOutput, calls=%fused_computation.17 | convolution fusion | flops 2149580800 | bytes 10485760 | tf_op jit(solution)/shard_map/end,emd->enm/dot_general | solution.py:27
  166.0 4.6 %fusion.1 = f32[2,512,64]{2,1,0:T(8,128)S(1)} fusion(f32[2,512,2048]{2,1,0:T(8,128)} %multiply_add_fusion.2, f32[2,2048]{1,0:T(2,128)S(1)} %copy-done.4, bf16[2048,64]{0,1:T(8,128)(2,1)S(1)} %copy-done), kind=kOutput, calls=%fused_computation.13 | convolution fusion | flops 272629760 | bytes 8929280 | tf_op jit(solution)/shard_map/end,dr->enr/dot_general | solution.py:26
  170.7 32.8 %all-reduce.13 = bf16[2,512,64]{2,1,0:T(8,128)(2,1)S(1)} all-reduce(f32[2,512,64]{2,1,0:T(8,128)S(1)} %fusion.1), channel_id=1, replica_groups=mesh['ens'=2,'feat'=8] {'feat'}, use_global_device_ids=true, to_apply=%region_4.5 | all-reduce | flops 65536 | bytes 393216 | tf_op jit(solution)/shard_map/psum | solution.py:28
  203.5 21.5 %all-reduce.9.cloned.1.call-done = f32[2,512,512]{2,1,0:T(8,128)} async-done(((f32[2,512,512]{2,1,0:T(8,128)}), f32[2,512,512]{2,1,0:T(8,128)}) %all-reduce.9.cloned.1.call-update) | async-done | bytes 2097168 | tf_op jit(solution)/shard_map/psum | solution.py:28
  225.0 60.2 %copy.17 = f32[2,512,512]{0,2,1:T(8,128)} copy(f32[2,512,512]{2,1,0:T(8,128)} %all-reduce.9.cloned.1.call-done) | data formatting | bytes 4194304 | tf_op jit(solution)/shard_map/psum | solution.py:28
  285.3 5.5 %gather_fusion.1 = f32[512,2]{1,0:T(8,128)S(1)} fusion(f32[2,512,512]{0,2,1:T(8,128)} %copy.17, s32[512]{0:T(512)S(1)} %bitcast.24), kind=kCustom, calls=%fused_computation.1 | custom fusion | bytes 12288 | tf_op jit(solution)/shard_map/jit(diagonal)/gather | solution.py:29
  290.9 0.8 fusion.14
  291.7 12.9 %multiply_add_fusion.1 = f32[2,512,2048]{2,1,0:T(8,128)} fusion(f32[2,512,2048]{2,1,0:T(8,128)} %multiply_add_fusion.2, f32[2,512]{1,0:T(2,128)S(1)} %broadcast_multiply_fusion.1, f32[2048]{0:T(1024)S(1)} %copy-done.5, f32[2,2048]{1,0:T(2,128)S(1)} %copy-done.4, f32[2,512,512]{2,1,0:T(8,128)S(1)} %copy-done.2, f32[2,512]{1,0:T(2,128)S(1)} %copy.18, ...), kind=kOutput, calls=%fused_computation.5 | convolution fusion | flops 2442657792 | bytes 19300352 | tf_op jit(solution)/shard_map/enm,emd->end/dot_general | solution.py:35
  304.7 9.4 %fusion.3 = f32[2,512,512]{2,1,0:T(8,128)} fusion(f32[2,512,2048]{2,1,0:T(8,128)} %multiply_add_fusion.1), kind=kOutput, calls=%fused_computation.15 | convolution fusion | flops 2149580800 | bytes 10485760 | tf_op jit(solution)/shard_map/end,emd->enm/dot_general | solution.py:27
  314.2 4.6 %fusion.2 = f32[2,512,64]{2,1,0:T(8,128)S(1)} fusion(f32[2,512,2048]{2,1,0:T(8,128)} %multiply_add_fusion.1, f32[2,2048]{1,0:T(2,128)S(1)} %copy-done.4, bf16[2048,64]{0,1:T(8,128)(2,1)S(1)} %copy-done), kind=kOutput, calls=%fused_computation.14 | convolution fusion | flops 272629760 | bytes 8929280 | tf_op jit(solution)/shard_map/end,dr->enr/dot_general | solution.py:26
  318.8 32.9 %all-reduce.14 = bf16[2,512,64]{2,1,0:T(8,128)(2,1)S(1)} all-reduce(f32[2,512,64]{2,1,0:T(8,128)S(1)} %fusion.2), channel_id=1, replica_groups=mesh['ens'=2,'feat'=8] {'feat'}, use_global_device_ids=true, to_apply=%region_7.8 | all-reduce | flops 65536 | bytes 393216 | tf_op jit(solution)/shard_map/psum | solution.py:28
  351.7 21.5 %all-reduce.11.cloned.1.call-done = f32[2,512,512]{2,1,0:T(8,128)} async-done(((f32[2,512,512]{2,1,0:T(8,128)}), f32[2,512,512]{2,1,0:T(8,128)}) %all-reduce.11.cloned.1.call-update) | async-done | bytes 2097168 | tf_op jit(solution)/shard_map/psum | solution.py:28
  373.3 60.2 %copy.20 = f32[2,512,512]{0,2,1:T(8,128)} copy(f32[2,512,512]{2,1,0:T(8,128)} %all-reduce.11.cloned.1.call-done) | data formatting | bytes 4194304 | tf_op jit(solution)/shard_map/psum | solution.py:28
  433.5 5.5 %gather_fusion.2 = f32[512,2]{1,0:T(8,128)S(1)} fusion(f32[2,512,512]{0,2,1:T(8,128)} %copy.20, s32[512]{0:T(512)S(1)} %bitcast.25), kind=kCustom, calls=%fused_computation.2 | custom fusion | bytes 12288 | tf_op jit(solution)/shard_map/jit(diagonal)/gather | solution.py:29
  439.1 0.8 fusion.16
  439.9 12.7 %multiply_add_fusion = f32[2,512,2048]{2,1,0:T(8,128)} fusion(f32[2,512,2048]{2,1,0:T(8,128)} %multiply_add_fusion.1, f32[2,512]{1,0:T(2,128)S(1)} %broadcast_multiply_fusion, f32[2048]{0:T(1024)S(1)} %copy-done.5, f32[2,2048]{1,0:T(2,128)S(1)} %copy-done.4, f32[2,512,512]{2,1,0:T(8,128)S(1)} %copy-done.3, f32[2,512]{1,0:T(2,128)S(1)} %copy.21, ...), kind=kOutput, calls=%fused_computation.3 | convolution fusion | flops 2442657792 | bytes 19300352 | tf_op jit(solution)/shard_map/enm,emd->end/dot_general | solution.py:35
  (25 shorter events, 0.7 us)
Async XLA Ops:
  6.5 9.6 %copy-start = (bf16[2048,64]{0,1:T(8,128)(2,1)S(1)}, bf16[2048,64]{0,1:T(8,128)(2,1)}, u32[]{:S(2)}) copy-start(bf16[2048,64]{0,1:T(8,128)(2,1)} %param.7) | copy-start | bytes 786436
  6.6 9.6 %copy-start.4 = (f32[2,2048]{1,0:T(2,128)S(1)}, f32[2,2048]{1,0:T(2,128)}, u32[]{:S(2)}) copy-start(f32[2,2048]{1,0:T(2,128)} %param.5) | copy-start | bytes 49156
  6.6 70.2 %all-reduce.7.cloned.1.call-start = ((), (), s32[]{:S(2)}) async-start(), calls=%async_computation | async-start | bytes 4194304 | tf_op jit(solution)/shard_map/psum | solution.py:28
  16.1 208.9 %all-reduce.9.cloned.1.call-start = ((), (), s32[]{:S(2)}) async-start(), calls=%async_computation.1 | async-start | bytes 4194304 | tf_op jit(solution)/shard_map/psum | solution.py:28
  52.1 91.3 %copy-start.5 = (f32[2048]{0:T(1024)S(1)}, f32[2048]{0:T(1024)}, u32[]{:S(2)}) copy-start(f32[2048]{0:T(1024)} %param.6) | copy-start | bytes 24580
  76.7 65.9 %copy-start.1 = (f32[2,512,512]{2,1,0:T(8,128)S(1)}, f32[2,512,512]{2,1,0:T(8,128)}, u32[]{:S(2)}) copy-start(f32[2,512,512]{2,1,0:T(8,128)} %all-reduce.7.cloned.1.call-done) | copy-start | bytes 6291460
  166.0 207.3 %all-reduce.11.cloned.1.call-start = ((), (), s32[]{:S(2)}) async-start(), calls=%async_computation.2 | async-start | bytes 4194304 | tf_op jit(solution)/shard_map/psum | solution.py:28
  225.0 65.9 %copy-start.2 = (f32[2,512,512]{2,1,0:T(8,128)S(1)}, f32[2,512,512]{2,1,0:T(8,128)}, u32[]{:S(2)}) copy-start(f32[2,512,512]{2,1,0:T(8,128)} %all-reduce.9.cloned.1.call-done) | copy-start | bytes 6291460
  373.3 65.9 %copy-start.3 = (f32[2,512,512]{2,1,0:T(8,128)S(1)}, f32[2,512,512]{2,1,0:T(8,128)}, u32[]{:S(2)}) copy-start(f32[2,512,512]{2,1,0:T(8,128)} %all-reduce.11.cloned.1.call-done) | copy-start | bytes 6291460
Sparse Core Ops, SparseCore 0:
  16.2 60.4 all-reduce.6
  166.1 58.9 all-reduce.8
  314.3 58.9 all-reduce.10
where the time goes:
time: 467 us; the launch traced here: 459 us
  local copies, waits for them, and re-layouts  198 us (42%)
  blocking collectives  97 us (21%)
  matrix products  80.9 us (17%)
  waiting for transfers between devices  67.8 us (15%)
  between operations  13.3 us (3%)
    psum x3, local copies, waits for them, and re-layouts, local_steps(): project, gram_mat = lax.psum((proj_part, gram_part), 'feat')  181 us
    psum x3, blocking collectives, local_steps(): project, gram_mat = lax.psum((proj_part, gram_part), 'feat')  97 us
    psum x3, waiting for transfers between devices, local_steps(): project, gram_mat = lax.psum((proj_part, gram_part), 'feat')  67.7 us
    dot_general x3, matrix products, local_steps(): jnp.einsum('enm,emd->end', kernel.astype(jnp.bfloat16), mixed, preferred_...  38.6 us
    dot_general x3, matrix products, local_steps(): jnp.einsum('end,emd->enm', theta_bf, theta_bf, preferred_element_type=jnp...  28.4 us
    gather x6, local copies, waits for them, and re-layouts, local_steps(): gram_diag = jnp.diagonal(gram_mat, axis1=1, axis2=2)  16.9 us
    dot_general x3, matrix products, local_steps(): jnp.einsum('end,dr->enr', centered.astype(jnp.bfloat16), low_factor, pref...  13.9 us
  transfers between devices with their start and end apart: 3, of which 3 were waited for; matrix products, arithmetic and copies ran while one was open for 3% of the time, Pallas kernels for 0%

commit v1 on v0

v1 whole, which is shorter than its diff:
```python
import functools

import jax
import jax.numpy as jnp
from jax import lax
from jax.experimental import pallas as pl
from jax.experimental.pallas import tpu as pltpu
from jax.sharding import PartitionSpec as P

NUM_STEPS = 3
MESH = pl.DeviceIdType.MESH
NT = (((1,), (1,)), ((), ()))
CHUNKS = 4
TILE = 512
VMEM_LIMIT = 60 * 1024 * 1024


def dot_nt(a, b):
    return lax.dot_general(a, b, NT, preferred_element_type=jnp.float32)


def exchange_kernel(cores, chips, part_hbm, mean_ref, prec_ref, low_ref,
                    theta_hbm, kern_out, proj_out, sums_out,
                    theta, theta_bf, drift, factor2, kern, proj, sums, proj_part, gram,
                    gbuf, dbuf, gsib, dsib, acc, dacc, gpeer, dpeer, kbuf, sbuf,
                    load_sem, store_sem, s1_send, s1_recv, s2_send, s2_recv, s3_send, s3_recv, s4_send, s4_recv):
    num_ens, num_part, loc_feat = theta.shape
    half = num_part // 2
    core_rows = half // cores
    piece = core_rows // chips
    bandwidth = 2.0 * loc_feat * cores * chips
    step_size = 0.25 * loc_feat * cores * chips

    me = lax.axis_index("feat")
    core = lax.rem(me, cores)
    chip = lax.div(me, cores)
    sibling = chip * cores + (1 - core)
    my_core_row = pl.multiple_of(core * core_rows, core_rows)
    sib_core_row = pl.multiple_of((1 - core) * core_rows, core_rows)
    my_piece_row = pl.multiple_of(my_core_row + chip * piece, piece)

    def chip_at(offset):
        return lax.rem(chip + offset, chips)

    def peer(offset):
        return chip_at(offset) * cores + core

    def remote(src, dst, send, recv, dev):
        return pltpu.make_async_remote_copy(src_ref=src, dst_ref=dst, send_sem=send, recv_sem=recv,
                                            device_id={"feat": dev}, device_id_type=MESH)

    rows = num_part // CHUNKS
    loads = {}
    for e in range(num_ens):
        for c in range(CHUNKS):
            loads[e, c] = pltpu.make_async_copy(part_hbm.at[e, pl.ds(c * rows, rows)],
                                                theta.at[e, pl.ds(c * rows, rows)], load_sem.at[e * CHUNKS + c])
            loads[e, c].start()

    barrier = pltpu.get_barrier_semaphore()
    for offset in range(1, cores * chips):
        pl.semaphore_signal(barrier, inc=1, device_id={"feat": lax.rem(me + offset, cores * chips)}, device_id_type=MESH)

    factor2[...] = jnp.concatenate([low_ref[...], low_ref[...]], axis=1)
    rank2 = factor2.shape[1]
    rank = rank2 // 2
    lane_low = lax.broadcasted_iota(jnp.int32, (half, rank2), 1) < rank
    row_id = lax.broadcasted_iota(jnp.int32, (half, half), 0)
    col_id = lax.broadcasted_iota(jnp.int32, (half, half), 1)

    def first_rows(e):
        for c in range(CHUNKS):
            loads[e, c].wait()
            sl = pl.ds(c * rows, rows)
            th = theta[e, sl, :]
            theta_bf[e, sl, :] = th.astype(jnp.bfloat16)
            xb = (th - mean_ref[e:e + 1, :]).astype(jnp.bfloat16)
            proj_part[e, sl, :] = jnp.dot(xb, factor2[...], preferred_element_type=jnp.float32)

    def gram_and_pack(e):
        gram[...] = dot_nt(theta_bf[e], theta_bf[e])
        g00 = gram[0:half, 0:half]
        g11 = gram[half:, half:]
        gbuf[e, :, 0:half] = jnp.where(col_id >= row_id, g00, g11)
        gbuf[e, :, half:2 * half] = gram[0:half, half:]
        gbuf[e, :, 2 * half:] = jnp.where(lane_low, proj_part[e, 0:half, :], proj_part[e, half:, :])
        d0 = jnp.sum(jnp.where(col_id == row_id, g00, 0.0), axis=0, keepdims=True)
        d1 = jnp.sum(jnp.where(col_id == row_id, g11, 0.0), axis=0, keepdims=True)
        dbuf[e] = jnp.concatenate([d0, d1, jnp.zeros((6, half), jnp.float32)], axis=0)

    def s1(e):
        return (remote(gbuf.at[e, pl.ds(sib_core_row, core_rows)], gsib.at[e], s1_send.at[2 * e], s1_recv.at[2 * e], sibling),
                remote(dbuf.at[e], dsib.at[e], s1_send.at[2 * e + 1], s1_recv.at[2 * e + 1], sibling))

    def s2(e, k):
        i = 2 * (e * chips + k)
        return (remote(acc.at[e, pl.ds(pl.multiple_of(chip_at(k) * piece, piece), piece)], gpeer.at[e, k - 1],
                       s2_send.at[i], s2_recv.at[i], peer(k)),
                remote(dacc.at[e], dpeer.at[e, k - 1], s2_send.at[i + 1], s2_recv.at[i + 1], peer(k)))

    def s3(e, k):
        i = 2 * (e * chips + k)
        mine = pl.ds(my_piece_row, piece)
        return (remote(kbuf.at[e, mine], kbuf.at[e, mine], s3_send.at[i], s3_recv.at[i], peer(k)),
                remote(sbuf.at[e, core * chips + chip], sbuf.at[e, core * chips + chip],
                       s3_send.at[i + 1], s3_recv.at[i + 1], peer(k)))

    def s3_in(e, k):
        i = 2 * (e * chips + k)
        src = chip_at(chips - k)
        rws = pl.ds(pl.multiple_of(my_core_row + src * piece, piece), piece)
        return (remote(kbuf.at[e, rws], kbuf.at[e, rws], s3_send.at[i], s3_recv.at[i], peer(chips - k)),
                remote(sbuf.at[e, core * chips + src], sbuf.at[e, core * chips + src],
                       s3_send.at[i + 1], s3_recv.at[i + 1], peer(chips - k)))

    def s4(e, k, owner_core):
        i = 2 * (e * chips + k)
        src = chip_at(chips - k)
        rws = pl.ds(pl.multiple_of(owner_core * core_rows + src * piece, piece), piece)
        return (remote(kbuf.at[e, rws], kbuf.at[e, rws], s4_send.at[i], s4_recv.at[i], sibling),
                remote(sbuf.at[e, owner_core * chips + src], sbuf.at[e, owner_core * chips + src],
                       s4_send.at[i + 1], s4_recv.at[i + 1], sibling))

    pending = {}

    def send(key, copies):
        for c in copies:
            c.start()
        pending.setdefault(key, []).extend(copies)

    def drain(key):
        for c in pending.pop(key, []):
            c.wait_send()

    def start_s1(e):
        send(("s1", e), s1(e))

    def mid_s1(e):
        for c in s1(e):
            c.wait_recv()
        drain(("s2", e))
        acc[e] = gbuf[e, pl.ds(my_core_row, core_rows), :] + gsib[e]
        dacc[e] = dbuf[e] + dsib[e]
        drain(("s1", e))
        for k in range(1, chips):
            send(("s2", e), s2(e, k))

    def mid_s2(e):
        for k in range(1, chips):
            for c in s2(e, k):
                c.wait_recv()
        own = acc[e, pl.ds(pl.multiple_of(chip * piece, piece), piece), :]
        dg = dacc[e]
        for k in range(1, chips):
            own = own + gpeer[e, k - 1]
            dg = dg + dpeer[e, k - 1]
        l0 = dg[0:1, :]
        l1 = dg[1:2, :]
        col = lax.broadcasted_iota(jnp.int32, (piece, half), 1)
        row = lax.broadcasted_iota(jnp.int32, (piece, half), 0) + my_piece_row
        on = col == row
        up = col >= row
        c0 = jnp.sum(jnp.where(on, l0, 0.0), axis=1, keepdims=True)
        c1 = jnp.sum(jnp.where(on, l1, 0.0), axis=1, keepdims=True)
        dist_t = jnp.maximum(jnp.where(up, c0 + l0, c1 + l1) - 2.0 * own[:, 0:half], 0.0)
        dist_o = jnp.maximum((c0 + l1) - 2.0 * own[:, half:2 * half], 0.0)
        k_t = jnp.where(on, 1.0, jnp.exp(-dist_t / bandwidth))
        k_o = jnp.exp(-dist_o / bandwidth)
        mine = pl.ds(my_piece_row, piece)
        kbuf[e, mine, 0:half] = k_t.astype(jnp.bfloat16)
        kbuf[e, mine, half:2 * half] = k_o.astype(jnp.bfloat16)
        kbuf[e, mine, 2 * half:] = own[:, 2 * half:].astype(jnp.bfloat16)
        low = col < row
        row0 = jnp.sum(jnp.where(up, k_t, 0.0) + k_o, axis=1, keepdims=True)
        row1 = jnp.sum(jnp.where(low, k_t, 0.0), axis=1, keepdims=True) + 1.0
        s0 = jnp.sum(jnp.where(col > row, k_t, 0.0) + jnp.where(on, row0, 0.0), axis=0, keepdims=True)
        s1_ = jnp.sum(jnp.where(low, k_t, 0.0) + k_o + jnp.where(on, row1, 0.0), axis=0, keepdims=True)
        sbuf[e, core * chips + chip] = jnp.concatenate([s0, s1_, jnp.zeros((6, half), jnp.float32)], axis=0)
        for k in range(1, chips):
            send(("s3", e), s3(e, k))
        send(("s4", e), s4(e, 0, core))

    def mid_s3(e):
        for k in sorted(range(1, chips), key=lambda k: min(k, chips - k)):
            for c in s3_in(e, k):
                c.wait_recv()
            send(("s4", e), s4(e, k, core))

    def unpack(e, kern_ref, proj_ref, sums_ref):
        for k in range(chips):
            for c in s4(e, k, 1 - core):
                c.wait_recv()
        drain(("s3", e))
        drain(("s4", e))
        t = kbuf[e, :, 0:half].astype(jnp.float32)
        tt = t.T
        kern_ref[0:half, 0:half] = jnp.where(col_id >= row_id, t, tt).astype(jnp.bfloat16)
        kern_ref[half:, half:] = jnp.where(col_id <= row_id, t, tt).astype(jnp.bfloat16)
        ko = kbuf[e, :, half:2 * half]
        kern_ref[0:half, half:] = ko
        kern_ref[half:, 0:half] = ko.astype(jnp.float32).T.astype(jnp.bfloat16)
        pj = kbuf[e, :, 2 * half:].astype(jnp.float32)
        proj_ref[0:half, :] = jnp.where(lane_low, pj, 0.0).astype(jnp.bfloat16)
        proj_ref[half:, :] = jnp.where(lane_low, 0.0, pj).astype(jnp.bfloat16)
        tot = sbuf[e, 0]
        for o in range(1, cores * chips):
            tot = tot + sbuf[e, o]
        tot = (2.0 / bandwidth) * tot
        for q in range(num_part // 128):
            r = q * 128 // half
            lo = q * 128 % half
            line = tot[r:r + 1, lo:lo + 128]
            sums_ref[pl.ds(q * 128, 128), :] = jnp.broadcast_to(line, (128, 128)).T

    def update(e):
        for t in range(loc_feat // TILE):
            sl = pl.ds(t * TILE, TILE)
            th = theta[e, :, sl]
            low = dot_nt(proj[...], factor2[sl, :])
            yn = (th - mean_ref[e:e + 1, sl]) * prec_ref[0:1, sl] + low + (2.0 / bandwidth) * th
            drift[...] = yn.astype(jnp.bfloat16)
            drive = jnp.dot(kern[...], drift[...], preferred_element_type=jnp.float32)
            srow = jnp.concatenate([sums[...]] * (TILE // 128), axis=1)
            new = th + step_size * ((srow * th - drive) / num_part)
            theta[e, :, sl] = new
            theta_bf[e, :, sl] = new.astype(jnp.bfloat16)
            xb = (new - mean_ref[e:e + 1, sl]).astype(jnp.bfloat16)
            part = jnp.dot(xb, factor2[sl, :], preferred_element_type=jnp.float32)
            if t == 0:
                proj_part[e] = part
            else:
                proj_part[e] += part

    first_rows(0)
    gram_and_pack(0)
    pl.semaphore_wait(barrier, cores * chips - 1)
    start_s1(0)
    first_rows(1)
    mid_s1(0)
    gram_and_pack(1)
    start_s1(1)
    stores = []
    for step in range(NUM_STEPS):
        mid_s1(1)
        mid_s2(0)
        mid_s2(1)
        mid_s3(0)
        if step < NUM_STEPS - 1:
            unpack(0, kern, proj, sums)
            update(0)
            mid_s3(1)
            gram_and_pack(0)
            start_s1(0)
            unpack(1, kern, proj, sums)
            update(1)
            mid_s1(0)
            gram_and_pack(1)
            start_s1(1)
            if step == NUM_STEPS - 2:
                for e in range(num_ens):
                    st = pltpu.make_async_copy(theta.at[e], theta_hbm.at[e], store_sem.at[e])
                    st.start()
                    stores.append(st)
        else:
            unpack(0, kern_out.at[0], proj_out.at[0], sums_out.at[0])
            mid_s3(1)
            unpack(1, kern_out.at[1], proj_out.at[1], sums_out.at[1])
    for st in stores:
        st.wait()
    for key in list(pending):
        drain(key)


def final_kernel(bandwidth, step_size, num_part, th_ref, kern_ref, proj_ref, sums_ref, mean_ref, prec_ref, low_ref, out_ref):
    th = th_ref[0]
    width = th.shape[1]
    low_t = low_ref[...]
    low = dot_nt(proj_ref[0], jnp.concatenate([low_t, low_t], axis=1))
    yn = (th - mean_ref[0]) * prec_ref[...] + low + (2.0 / bandwidth) * th
    drive = jnp.dot(kern_ref[0], yn.astype(jnp.bfloat16), preferred_element_type=jnp.float32)
    srow = jnp.concatenate([sums_ref[0]] * (width // 128), axis=1)
    out_ref[0] = th + step_size * ((srow * th - drive) / num_part)


def solution(mesh):
    feat_count = mesh.shape["feat"]
    cores = 2
    chips = feat_count // cores
    data_spec = P("ens", None, "feat")
    mean_spec = P("ens", "feat")
    prec_spec = P(("ens", "feat"))
    factor_spec = P(("ens", "feat"), None)

    def local_steps(particles, target_mean, precision, low_factor):
        num_ens, num_part, loc_feat = particles.shape
        rank = low_factor.shape[1]
        half = num_part // 2
        core_rows = half // cores
        piece = core_rows // chips
        width = 2 * half + 2 * rank
        bandwidth = 2.0 * loc_feat * feat_count
        step_size = 0.25 * loc_feat * feat_count
        prec_row = precision.reshape(1, loc_feat)
        f32, bf16 = jnp.float32, jnp.bfloat16
        vmem = pl.BlockSpec(memory_space=pltpu.VMEM)
        anyspace = pl.BlockSpec(memory_space=pl.ANY)
        dma = pltpu.SemaphoreType.DMA
        nsem = 2 * num_ens * chips
        theta, kern, proj, sums = pl.pallas_call(
            functools.partial(exchange_kernel, cores, chips),
            out_shape=(
                jax.ShapeDtypeStruct((num_ens, num_part, loc_feat), f32),
                jax.ShapeDtypeStruct((num_ens, num_part, num_part), bf16),
                jax.ShapeDtypeStruct((num_ens, num_part, 2 * rank), bf16),
                jax.ShapeDtypeStruct((num_ens, num_part, 128), f32),
            ),
            in_specs=[anyspace, vmem, vmem, vmem],
            out_specs=(anyspace, vmem, vmem, vmem),
            scratch_shapes=[
                pltpu.VMEM((num_ens, num_part, loc_feat), f32),
                pltpu.VMEM((num_ens, num_part, loc_feat), bf16),
                pltpu.VMEM((num_part, TILE), bf16),
                pltpu.VMEM((loc_feat, 2 * rank), bf16),
                pltpu.VMEM((num_part, num_part), bf16),
                pltpu.VMEM((num_part, 2 * rank), bf16),
                pltpu.VMEM((num_part, 128), f32),
                pltpu.VMEM((num_ens, num_part, 2 * rank), f32),
                pltpu.VMEM((num_part, num_part), f32),
                pltpu.VMEM((num_ens, half, width), f32),
                pltpu.VMEM((num_ens, 8, half), f32),
                pltpu.VMEM((num_ens, core_rows, width), f32),
                pltpu.VMEM((num_ens, 8, half), f32),
                pltpu.VMEM((num_ens, core_rows, width), f32),
                pltpu.VMEM((num_ens, 8, half), f32),
                pltpu.VMEM((num_ens, chips - 1, piece, width), f32),
                pltpu.VMEM((num_ens, chips - 1, 8, half), f32),
                pltpu.VMEM((num_ens, half, width), bf16),
                pltpu.VMEM((num_ens, feat_count, 8, half), f32),
                dma((num_ens * CHUNKS,)),
                dma((num_ens,)),
                dma((2 * num_ens,)), dma((2 * num_ens,)),
                dma((nsem,)), dma((nsem,)),
                dma((nsem,)), dma((nsem,)),
                dma((nsem,)), dma((nsem,)),
            ],
            compiler_params=pltpu.CompilerParams(
                collective_id=0, has_side_effects=True, vmem_limit_bytes=VMEM_LIMIT),
            name="exchange",
        )(particles, target_mean, prec_row, low_factor)
        tiles = loc_feat // TILE
        return pl.pallas_call(
            functools.partial(final_kernel, bandwidth, step_size, num_part),
            out_shape=jax.ShapeDtypeStruct((num_ens, num_part, loc_feat), f32),
            grid=(num_ens, tiles),
            in_specs=[
                pl.BlockSpec((1, num_part, TILE), lambda e, t: (e, 0, t)),
                pl.BlockSpec((1, num_part, num_part), lambda e, t: (e, 0, 0)),
                pl.BlockSpec((1, num_part, 2 * rank), lambda e, t: (e, 0, 0)),
                pl.BlockSpec((1, num_part, 128), lambda e, t: (e, 0, 0)),
                pl.BlockSpec((1, 1, TILE), lambda e, t: (e, 0, t)),
                pl.BlockSpec((1, TILE), lambda e, t: (0, t)),
                pl.BlockSpec((TILE, rank), lambda e, t: (t, 0)),
            ],
            out_specs=pl.BlockSpec((1, num_part, TILE), lambda e, t: (e, 0, t)),
            name="final_update",
        )(theta, kern, proj, sums, target_mean[:, None, :], prec_row, low_factor)

    return jax.shard_map(local_steps, mesh=mesh, in_specs=(data_spec, mean_spec, prec_spec, factor_spec),
                         out_specs=data_spec, check_vma=False)
```

time: 467 us -> 85.4 us (0.18); the launches traced: 459 us -> 85 us
  local copies, waits for them, and re-layouts: 198 us -> 3.28 us
  blocking collectives: 97 us -> 0 us
  Pallas kernels: 0 us -> 81.7 us
  matrix products: 80.9 us -> 0 us
  waiting for transfers between devices: 67.8 us -> 0 us
  between operations: 13.3 us -> 0.01 us
    psum x3 -> x0, local copies, waits for them, and re-layouts: 181 us -> none  [local_steps(): project, gram_mat = lax.psum((proj_part, gram_part), 'feat')]
    psum x3 -> x0, blocking collectives: 97 us -> none  [local_steps(): project, gram_mat = lax.psum((proj_part, gram_part), 'feat')]
    pallas_call x0 -> x2, Pallas kernels: none -> 81.7 us  [the longest x1 69.7 us: local_steps(): pl.pallas_call(functools.partial(exchange_kernel, cores, chips), out_shap...]
    dot_general x9 -> x0, matrix products: 80.9 us -> none  [the longest x3 38.6 us: local_steps(): jnp.einsum('enm,emd->end', kernel.astype(jnp.bfloat16), mixed, preferred_...]
    psum x3 -> x0, waiting for transfers between devices: 67.7 us -> none  [local_steps(): project, gram_mat = lax.psum((proj_part, gram_part), 'feat')]
    gather x6 -> x0, local copies, waits for them, and re-layouts: 16.9 us -> none  [local_steps(): gram_diag = jnp.diagonal(gram_mat, axis1=1, axis2=2)]
  transfers between devices with their start and end apart: 3 -> 0, of which waited for: 3 -> 0; matrix products, arithmetic and copies ran while one was open for 3% -> 0% of each run, Pallas kernels for 0% -> 0%
where the time goes in v1:
time: 85.4 us; the launch traced here: 85 us
  Pallas kernels  81.7 us (96%)
  local copies, waits for them, and re-layouts  3.28 us (4%)
    pallas_call x1, Pallas kernels, local_steps(): pl.pallas_call(functools.partial(exchange_kernel, cores, chips), out_shap...  69.7 us
    pallas_call x1, Pallas kernels, local_steps(): pl.pallas_call(functools.partial(final_kernel, bandwidth, step_size, num_...  12 us
    unnamed x1, local copies, waits for them, and re-layouts  1.96 us

profile of v1, /device:TPU:113, one launch (start us, length us, event | category | flops | bytes accessed | tf_op | source)
XLA Modules:
  0.0 85.0 jit_solution(8880615536366047322)
XLA Ops:
  0.0 1.3 %broadcast_in_dim.3.mean_ref = f32[2,1,2048]{2,1,0:T(1,128)} reshape(f32[2,2048]{1,0:T(2,128)} %mean_ref.1) | data formatting | bytes 32768 | tf_op jit(solution)/shard_map/broadcast_in_dim | solution.py:366
  1.3 2.0 %copy.5.low_ref = bf16[2048,64]{1,0:T(8,128)(2,1)} copy(bf16[2048,64]{0,1:T(8,128)(2,1)} %param.7) | data formatting | bytes 524288 | tf_op args[3]
  3.3 69.7 %exchange.1 = (f32[2,512,2048]{2,1,0:T(8,128)}, bf16[2,512,512]{2,1,0:T(8,128)(2,1)}, bf16[2,512,128]{2,1,0:T(8,128)(2,1)}, f32[2,512,128]{2,1,0:T(8,128)}) custom-call(f32[2,512,2048]{2,1,0:T(8,128)} %part_hbm.1, f32[2,2048]{1,0:T(2,128)} %mean_ref.1, f32[1,2048]{1,0:T(1,128)} %bitcast.1, bf16[2048,64]{1,0:T(8,128)(2,1)} %copy.5.low_ref), custom_call_target="tpu_custom_call" | custom-call | tf_op jit(solution)/shard_map/exchange/pallas_call | solution.py:309
  73.0 12.0 %final_update.1 = f32[2,512,2048]{2,1,0:T(8,128)} custom-call(f32[2,512,2048]{2,1,0:T(8,128)} %get-tuple-element.9.th_ref, bf16[2,512,512]{2,1,0:T(8,128)(2,1)} %get-tuple-element.10.kern_ref, bf16[2,512,128]{2,1,0:T(8,128)(2,1)} %get-tuple-element.11.proj_ref, f32[2,512,128]{2,1,0:T(8,128)} %get-tuple-element.12.sums_ref, ...), custom_call_target="tpu_custom_call" | custom-call | tf_op jit(solution)/shard_map/final_update/pallas_call | solution.py:351

commit v2 on v1

--- a/solution.py
+++ b/solution.py
@@ -12,18 +12,27 @@
 NT = (((1,), (1,)), ((), ()))
 CHUNKS = 4
 TILE = 512
-VMEM_LIMIT = 60 * 1024 * 1024
+VMEM_LIMIT = 40 * 1024 * 1024
+FINAL_LIMIT = 20 * 1024 * 1024
 
 
 def dot_nt(a, b):
     return lax.dot_general(a, b, NT, preferred_element_type=jnp.float32)
 
 
+def advance(th, kern, proj, sums, mean, prec, fact, bandwidth, step_size, num_part):
+    low = jnp.dot(proj[...], fact, preferred_element_type=jnp.float32)
+    yn = (th - mean) * prec + low + (2.0 / bandwidth) * th
+    drive = jnp.dot(kern[...], yn.astype(jnp.bfloat16), preferred_element_type=jnp.float32)
+    srow = jnp.concatenate([sums[...]] * (th.shape[1] // 128), axis=1)
+    return th + step_size * ((srow * th - drive) / num_part)
+
+
 def exchange_kernel(cores, chips, part_hbm, mean_ref, prec_ref, low_ref,
-                    theta_hbm, kern_out, proj_out, sums_out,
-                    theta, theta_bf, drift, factor2, kern, proj, sums, proj_part, gram,
+                    theta, kern_out, proj_out, sums_out,
+                    theta_bf, factor2, kern, proj, sums, proj_part, gram,
                     gbuf, dbuf, gsib, dsib, acc, dacc, gpeer, dpeer, kbuf, sbuf,
-                    load_sem, store_sem, s1_send, s1_recv, s2_send, s2_recv, s3_send, s3_recv, s4_send, s4_recv):
+                    load_sem, s1_send, s1_recv, s2_send, s2_recv, s3_send, s3_recv, s4_send, s4_recv):
     num_ens, num_part, loc_feat = theta.shape
     half = num_part // 2
     core_rows = half // cores
@@ -61,8 +70,8 @@
     for offset in range(1, cores * chips):
         pl.semaphore_signal(barrier, inc=1, device_id={"feat": lax.rem(me + offset, cores * chips)}, device_id_type=MESH)
 
-    factor2[...] = jnp.concatenate([low_ref[...], low_ref[...]], axis=1)
-    rank2 = factor2.shape[1]
+    factor2[...] = jnp.concatenate([low_ref[...], low_ref[...]], axis=0)
+    rank2 = factor2.shape[0]
     rank = rank2 // 2
     lane_low = lax.broadcasted_iota(jnp.int32, (half, rank2), 1) < rank
     row_id = lax.broadcasted_iota(jnp.int32, (half, half), 0)
@@ -75,7 +84,7 @@
             th = theta[e, sl, :]
             theta_bf[e, sl, :] = th.astype(jnp.bfloat16)
             xb = (th - mean_ref[e:e + 1, :]).astype(jnp.bfloat16)
-            proj_part[e, sl, :] = jnp.dot(xb, factor2[...], preferred_element_type=jnp.float32)
+            proj_part[e, sl, :] = dot_nt(xb, factor2[...])
 
     def gram_and_pack(e):
         gram[...] = dot_nt(theta_bf[e], theta_bf[e])
@@ -212,20 +221,17 @@
             line = tot[r:r + 1, lo:lo + 128]
             sums_ref[pl.ds(q * 128, 128), :] = jnp.broadcast_to(line, (128, 128)).T
 
-    def update(e):
+    def update(e, last):
         for t in range(loc_feat // TILE):
             sl = pl.ds(t * TILE, TILE)
-            th = theta[e, :, sl]
-            low = dot_nt(proj[...], factor2[sl, :])
-            yn = (th - mean_ref[e:e + 1, sl]) * prec_ref[0:1, sl] + low + (2.0 / bandwidth) * th
-            drift[...] = yn.astype(jnp.bfloat16)
-            drive = jnp.dot(kern[...], drift[...], preferred_element_type=jnp.float32)
-            srow = jnp.concatenate([sums[...]] * (TILE // 128), axis=1)
-            new = th + step_size * ((srow * th - drive) / num_part)
+            new = advance(theta[e, :, sl], kern, proj, sums, mean_ref[e:e + 1, sl], prec_ref[0:1, sl],
+                          factor2[:, sl], bandwidth, step_size, num_part)
             theta[e, :, sl] = new
+            if last:
+                continue
             theta_bf[e, :, sl] = new.astype(jnp.bfloat16)
             xb = (new - mean_ref[e:e + 1, sl]).astype(jnp.bfloat16)
-            part = jnp.dot(xb, factor2[sl, :], preferred_element_type=jnp.float32)
+            part = dot_nt(xb, factor2[:, sl])
             if t == 0:
                 proj_part[e] = part
             else:
@@ -239,47 +245,47 @@
     mid_s1(0)
     gram_and_pack(1)
     start_s1(1)
-    stores = []
     for step in range(NUM_STEPS):
+        last = step == NUM_STEPS - 1
         mid_s1(1)
         mid_s2(0)
         mid_s2(1)
         mid_s3(0)
-        if step < NUM_STEPS - 1:
-            unpack(0, kern, proj, sums)
-            update(0)
+        unpack(0, kern, proj, sums)
+        if last:
+            mid_s3(1)
+            update(0, True)
+            unpack(1, kern_out, proj_out, sums_out)
+        else:
+            update(0, False)
             mid_s3(1)
             gram_and_pack(0)
             start_s1(0)
             unpack(1, kern, proj, sums)
-            update(1)
+            update(1, False)
             mid_s1(0)
             gram_and_pack(1)
             start_s1(1)
-            if step == NUM_STEPS - 2:
-                for e in range(num_ens):
-                    st = pltpu.make_async_copy(theta.at[e], theta_hbm.at[e], store_sem.at[e])
-                    st.start()
-                    stores.append(st)
-        else:
-            unpack(0, kern_out.at[0], proj_out.at[0], sums_out.at[0])
-            mid_s3(1)
-            unpack(1, kern_out.at[1], proj_out.at[1], sums_out.at[1])
+    for key in list(pending):
+        drain(key)
+
+
+def final_kernel(bandwidth, step_size, theta, kern, proj, sums, mean_ref, prec_ref, low_ref, out_hbm, done, store_sem):
+    num_ens, num_part, loc_feat = theta.shape
+    stores = []
+    for e in range(num_ens - 1):
+        stores.append(pltpu.make_async_copy(theta.at[e], out_hbm.at[e], store_sem.at[e]))
+        stores[-1].start()
+    e = num_ens - 1
+    for t in range(loc_feat // TILE):
+        sl = pl.ds(t * TILE, TILE)
+        low_t = low_ref[:, sl]
+        done[t] = advance(theta[e, :, sl], kern, proj, sums, mean_ref[e:e + 1, sl], prec_ref[0:1, sl],
+                          jnp.concatenate([low_t, low_t], axis=0), bandwidth, step_size, num_part)
+        stores.append(pltpu.make_async_copy(done.at[t], out_hbm.at[e, :, sl], store_sem.at[e + t]))
+        stores[-1].start()
     for st in stores:
         st.wait()
-    for key in list(pending):
-        drain(key)
-
-
-def final_kernel(bandwidth, step_size, num_part, th_ref, kern_ref, proj_ref, sums_ref, mean_ref, prec_ref, low_ref, out_ref):
-    th = th_ref[0]
-    width = th.shape[1]
-    low_t = low_ref[...]
-    low = dot_nt(proj_ref[0], jnp.concatenate([low_t, low_t], axis=1))
-    yn = (th - mean_ref[0]) * prec_ref[...] + low + (2.0 / bandwidth) * th
-    drive = jnp.dot(kern_ref[0], yn.astype(jnp.bfloat16), preferred_element_type=jnp.float32)
-    srow = jnp.concatenate([sums_ref[0]] * (width // 128), axis=1)
-    out_ref[0] = th + step_size * ((srow * th - drive) / num_part)
 
 
 def solution(mesh):
@@ -301,6 +307,7 @@
         bandwidth = 2.0 * loc_feat * feat_count
         step_size = 0.25 * loc_feat * feat_count
         prec_row = precision.reshape(1, loc_feat)
+        low_t = low_factor.T
         f32, bf16 = jnp.float32, jnp.bfloat16
         vmem = pl.BlockSpec(memory_space=pltpu.VMEM)
         anyspace = pl.BlockSpec(memory_space=pl.ANY)
@@ -310,17 +317,15 @@
             functools.partial(exchange_kernel, cores, chips),
             out_shape=(
                 jax.ShapeDtypeStruct((num_ens, num_part, loc_feat), f32),
-                jax.ShapeDtypeStruct((num_ens, num_part, num_part), bf16),
-                jax.ShapeDtypeStruct((num_ens, num_part, 2 * rank), bf16),
-                jax.ShapeDtypeStruct((num_ens, num_part, 128), f32),
+                jax.ShapeDtypeStruct((num_part, num_part), bf16),
+                jax.ShapeDtypeStruct((num_part, 2 * rank), bf16),
+                jax.ShapeDtypeStruct((num_part, 128), f32),
             ),
             in_specs=[anyspace, vmem, vmem, vmem],
-            out_specs=(anyspace, vmem, vmem, vmem),
+            out_specs=(vmem, vmem, vmem, vmem),
             scratch_shapes=[
-                pltpu.VMEM((num_ens, num_part, loc_feat), f32),
                 pltpu.VMEM((num_ens, num_part, loc_feat), bf16),
-                pltpu.VMEM((num_part, TILE), bf16),
-                pltpu.VMEM((loc_feat, 2 * rank), bf16),
+                pltpu.VMEM((2 * rank, loc_feat), bf16),
                 pltpu.VMEM((num_part, num_part), bf16),
                 pltpu.VMEM((num_part, 2 * rank), bf16),
                 pltpu.VMEM((num_part, 128), f32),
@@ -337,7 +342,6 @@
                 pltpu.VMEM((num_ens, half, width), bf16),
                 pltpu.VMEM((num_ens, feat_count, 8, half), f32),
                 dma((num_ens * CHUNKS,)),
-                dma((num_ens,)),
                 dma((2 * num_ens,)), dma((2 * num_ens,)),
                 dma((nsem,)), dma((nsem,)),
                 dma((nsem,)), dma((nsem,)),
@@ -346,24 +350,17 @@
             compiler_params=pltpu.CompilerParams(
                 collective_id=0, has_side_effects=True, vmem_limit_bytes=VMEM_LIMIT),
             name="exchange",
-        )(particles, target_mean, prec_row, low_factor)
+        )(particles, target_mean, prec_row, low_t)
         tiles = loc_feat // TILE
         return pl.pallas_call(
-            functools.partial(final_kernel, bandwidth, step_size, num_part),
+            functools.partial(final_kernel, bandwidth, step_size),
             out_shape=jax.ShapeDtypeStruct((num_ens, num_part, loc_feat), f32),
-            grid=(num_ens, tiles),
-            in_specs=[
-                pl.BlockSpec((1, num_part, TILE), lambda e, t: (e, 0, t)),
-                pl.BlockSpec((1, num_part, num_part), lambda e, t: (e, 0, 0)),
-                pl.BlockSpec((1, num_part, 2 * rank), lambda e, t: (e, 0, 0)),
-                pl.BlockSpec((1, num_part, 128), lambda e, t: (e, 0, 0)),
-                pl.BlockSpec((1, 1, TILE), lambda e, t: (e, 0, t)),
-                pl.BlockSpec((1, TILE), lambda e, t: (0, t)),
-                pl.BlockSpec((TILE, rank), lambda e, t: (t, 0)),
-            ],
-            out_specs=pl.BlockSpec((1, num_part, TILE), lambda e, t: (e, 0, t)),
+            in_specs=[vmem] * 7,
+            out_specs=anyspace,
+            scratch_shapes=[pltpu.VMEM((tiles, num_part, TILE), f32), dma((num_ens - 1 + tiles,))],
+            compiler_params=pltpu.CompilerParams(vmem_limit_bytes=FINAL_LIMIT),
             name="final_update",
-        )(theta, kern, proj, sums, target_mean[:, None, :], prec_row, low_factor)
+        )(theta, kern, proj, sums, target_mean, prec_row, low_t)
 
     return jax.shard_map(local_steps, mesh=mesh, in_specs=(data_spec, mean_spec, prec_spec, factor_spec),
                          out_specs=data_spec, check_vma=False)

time: 85.4 us -> 75.6 us (0.89)
  Pallas kernels: 81.7 us -> 71.9 us
  local copies, waits for them, and re-layouts: 3.28 us -> 2.36 us
    pallas_call x1, Pallas kernels: 12 us -> 3.5 us  [local_steps(): pl.pallas_call(functools.partial(final_kernel, bandwidth, step_size), out...]
    broadcast_in_dim x1 -> x0, local copies, waits for them, and re-layouts: 1.32 us -> none  [local_steps(): target_mean[:, None, :]]
    pallas_call x1, Pallas kernels: 69.7 us -> 68.5 us  [local_steps(): pl.pallas_call(functools.partial(exchange_kernel, cores, chips), out_shap...]
    unnamed x1 -> x6, local copies, waits for them, and re-layouts: 1.96 us -> 2.36 us
where the time goes in v2:
time: 75.6 us; the launch traced here: 74.5 us
  Pallas kernels  71.9 us (95%)
  local copies, waits for them, and re-layouts  2.36 us (3%)
    pallas_call x1, Pallas kernels, local_steps(): pl.pallas_call(functools.partial(exchange_kernel, cores, chips), out_shap...  68.5 us
    pallas_call x1, Pallas kernels, local_steps(): pl.pallas_call(functools.partial(final_kernel, bandwidth, step_size), out...  3.5 us
    unnamed x6, local copies, waits for them, and re-layouts  2.36 us

profile of v2, /device:TPU:113, one launch (start us, length us, event | category | flops | bytes accessed | tf_op | source)
XLA Modules:
  0.0 74.5 jit_solution(10010508022663560310)
XLA Ops:
  0.0 0.0 copy-start
  0.0 0.9 %copy-done = bf16[2048,64]{0,1:T(8,128)(2,1)S(1)} copy-done((bf16[2048,64]{0,1:T(8,128)(2,1)S(1)}, bf16[2048,64]{0,1:T(8,128)(2,1)}, u32[]{:S(2)}) %copy-start) | copy-done | bytes 262168
  1.0 0.0 copy-start.1
  1.0 0.7 copy-done.1
  1.7 0.0 copy-start.2
  1.7 0.7 copy-done.2
  2.4 68.5 %exchange.1 = (f32[2,512,2048]{2,1,0:T(8,128)S(1)}, bf16[512,512]{1,0:T(8,128)(2,1)S(1)}, bf16[512,128]{1,0:T(8,128)(2,1)S(1)}, f32[512,128]{1,0:T(8,128)S(1)}) custom-call(f32[2,512,2048]{2,1,0:T(8,128)} %part_hbm.1, f32[2,2048]{1,0:T(2,128)S(1)} %copy-done.1, f32[1,2048]{1,0:T(1,128)S(1)} %bitcast.4, bf16[64,2048]{1,0:T(8,128)(2,1)S(1)} %bitcast.2), custom_call_target="tpu_custom_call" | custom-call | tf_op jit(solution)/shard_map/exchange/pallas_call | solution.py:316
  70.8 3.5 %final_update.1 = f32[2,512,2048]{2,1,0:T(8,128)} custom-call(f32[2,512,2048]{2,1,0:T(8,128)S(1)} %get-tuple-element.9.theta, bf16[512,512]{1,0:T(8,128)(2,1)S(1)} %get-tuple-element.10.kern, bf16[512,128]{1,0:T(8,128)(2,1)S(1)} %get-tuple-element.11.proj, f32[512,128]{1,0:T(8,128)S(1)} %get-tuple-element.12.sums, f32[2,2048]{1,0:T(2,128)S(1)} %copy-done.1, ...), custom_call_target="tpu_custom_call" | custom-call | tf_op jit(solution)/shard_map/final_update/pallas_call | solution.py:355
Async XLA Ops:
  0.0 0.9 %copy-start = (bf16[2048,64]{0,1:T(8,128)(2,1)S(1)}, bf16[2048,64]{0,1:T(8,128)(2,1)}, u32[]{:S(2)}) copy-start(bf16[2048,64]{0,1:T(8,128)(2,1)} %param.7) | copy-start | bytes 786436
  1.0 0.7 copy-start.1
  1.7 0.7 copy-start.2

commit v3 on v0

v3 whole, which is shorter than its diff:
```python
import functools

import jax
import jax.numpy as jnp
from jax import lax
from jax.experimental import pallas as pl
from jax.experimental.pallas import tpu as pltpu
from jax.sharding import PartitionSpec as P

NUM_STEPS = 3
MESH = pl.DeviceIdType.MESH
NT = (((1,), (1,)), ((), ()))
CHUNKS = 4
TILE = 512
LANES = 128
VMEM_LIMIT = 40 * 1024 * 1024
FINAL_LIMIT = 20 * 1024 * 1024


def dot_nt(a, b):
    return lax.dot_general(a, b, NT, preferred_element_type=jnp.float32)


def advance(th, kern, yn, sums, step_size, num_part):
    drive = jnp.dot(kern[...], yn, preferred_element_type=jnp.float32)
    srow = jnp.concatenate([sums[...]] * (th.shape[1] // LANES), axis=1)
    return th + step_size * ((srow * th - drive) / num_part)


def exchange_kernel(cores, chips, part_hbm, mean_hbm, prec_hbm, low_hbm,
                    theta, kern1, sums1, yn1,
                    theta_bf, mean, prec, factor, factor2, kern0, sums0, yn0, proj, proj_part, gram,
                    gbuf, gsib, acc, gpeer, kbuf, qbuf, qsib, qacc, qpeer, qall, dbuf, dpeer, sbuf,
                    load_sem, small_sem, g1s, g1r, g2s, g2r, g3s, g3r,
                    q1s, q1r, q2s, q2r, q3s, q3r, ds, dr, t3s, t3r):
    num_ens, num_part, loc_feat = theta.shape
    half = num_part // 2
    group = cores * chips
    core_rows = half // cores
    piece = core_rows // chips
    bandwidth = 2.0 * loc_feat * group
    step_size = 0.25 * loc_feat * group
    kern, sums, yn = (kern0, kern1), (sums0, sums1), (yn0, yn1)

    me = lax.axis_index("feat")
    core = lax.rem(me, cores)
    chip = lax.div(me, cores)
    sibling = chip * cores + (1 - core)
    my_rows = pl.ds(pl.multiple_of(core * core_rows, core_rows), core_rows)
    sib_rows = pl.ds(pl.multiple_of((1 - core) * core_rows, core_rows), core_rows)
    first_row = pl.multiple_of(core * core_rows + chip * piece, piece)
    my_piece = pl.ds(first_row, piece)
    own_rows = pl.ds(pl.multiple_of(chip * piece, piece), piece)

    def chip_at(offset):
        return lax.rem(chip + offset, chips)

    def peer(offset):
        return chip_at(offset) * cores + core

    def remote(src, dst, send, recv, dev):
        return pltpu.make_async_remote_copy(src_ref=src, dst_ref=dst, send_sem=send, recv_sem=recv,
                                            device_id={"feat": dev}, device_id_type=MESH)

    far_first = sorted(range(1, chips), key=lambda k: -min(k, chips - k))
    near_first = far_first[::-1]

    rows = num_part // CHUNKS
    smalls = [pltpu.make_async_copy(a, b, small_sem.at[i])
              for i, (a, b) in enumerate(((low_hbm, factor), (mean_hbm, mean), (prec_hbm, prec)))]
    for c in smalls:
        c.start()
    loads = {}
    for e in range(num_ens):
        for c in range(CHUNKS):
            loads[e, c] = pltpu.make_async_copy(part_hbm.at[e, pl.ds(c * rows, rows)],
                                                theta.at[e, pl.ds(c * rows, rows)], load_sem.at[e * CHUNKS + c])
    for c in range(CHUNKS):
        loads[0, c].start()

    barrier = pltpu.get_barrier_semaphore()
    for offset in range(1, group):
        pl.semaphore_signal(barrier, inc=1, device_id={"feat": lax.rem(me + offset, group)}, device_id_type=MESH)

    for c in smalls:
        c.wait()
    factor2[...] = jnp.concatenate([factor[...], factor[...]], axis=0)
    rank2 = factor2.shape[0]
    rank = rank2 // 2
    lane_low = lax.broadcasted_iota(jnp.int32, (half, rank2), 1) < rank
    row_id = lax.broadcasted_iota(jnp.int32, (half, half), 0)
    col_id = lax.broadcasted_iota(jnp.int32, (half, half), 1)

    def g1(e):
        return remote(gbuf.at[e, sib_rows], gsib.at[e], g1s.at[e], g1r.at[e], sibling)

    def q1(e):
        return remote(qbuf.at[e, sib_rows], qsib.at[e], q1s.at[e], q1r.at[e], sibling)

    def dg(e, o):
        i = e * group + o
        return remote(dbuf.at[e], dpeer.at[e, o - 1], ds.at[i], dr.at[i], lax.rem(me + o, group))

    def to_owner(src, dst, send, recv, e, k):
        i = e * chips + k
        return remote(src.at[e, pl.ds(pl.multiple_of(chip_at(k) * piece, piece), piece)], dst.at[e, k - 1],
                      send.at[i], recv.at[i], peer(k))

    def g2(e, k):
        return to_owner(acc, gpeer, g2s, g2r, e, k)

    def q2(e, k):
        return to_owner(qacc, qpeer, q2s, q2r, e, k)

    def rows_of(owner_core, owner_chip):
        return pl.ds(pl.multiple_of(owner_core * core_rows + owner_chip * piece, piece), piece)

    def core_of(other):
        return (1 - core) if other else core

    def out_of(buf, index, send, recv, e, k, other):
        i = 2 * (e * chips + k) + other
        return remote(buf.at[e, index], buf.at[e, index], send.at[i], recv.at[i], chip_at(k) * cores + core_of(other))

    def into(buf, lines, send, recv, e, k, other):
        i = 2 * (e * chips + k) + other
        src, src_core = chip_at(chips - k), core_of(other)
        index = src * cores + src_core if lines else rows_of(src_core, src)
        return remote(buf.at[e, index], buf.at[e, index], send.at[i], recv.at[i], src * cores + src_core)

    others = [(k, other) for k in far_first for other in (0, 1)] + [(0, 1)]

    def spread(key, buf, index, send_sem, recv_sem, e):
        for k, other in others:
            send((key, e), out_of(buf, index, send_sem, recv_sem, e, k, other))

    def gathered(buf, lines, send_sem, recv_sem, e):
        for k, other in others:
            into(buf, lines, send_sem, recv_sem, e, k, other).wait_recv()

    pending = {}

    def send(key, *copies):
        for c in copies:
            c.start()
        pending.setdefault(key, []).extend(copies)

    def drain(key):
        for c in pending.pop(key, []):
            c.wait_send()

    def first_rows(e):
        for c in range(CHUNKS):
            loads[e, c].wait()
            if e + 1 < num_ens:
                loads[e + 1, c].start()
            sl = pl.ds(c * rows, rows)
            th = theta[e, sl, :]
            theta_bf[e, sl, :] = th.astype(jnp.bfloat16)
            xb = (th - mean[e:e + 1, :]).astype(jnp.bfloat16)
            proj_part[e, sl, :] = dot_nt(xb, factor2[...])

    def send_q(e):
        qbuf[e] = jnp.where(lane_low, proj_part[e, 0:half, :], proj_part[e, half:, :])
        send(("q1", e), q1(e))

    def gram_and_send(e):
        gram[...] = dot_nt(theta_bf[e], theta_bf[e])
        g00 = gram[0:half, 0:half]
        g11 = gram[half:, half:]
        gbuf[e, :, 0:half] = jnp.where(col_id >= row_id, g00, g11)
        gbuf[e, :, half:2 * half] = gram[0:half, half:]
        send(("g1", e), g1(e))
        d0 = jnp.sum(jnp.where(col_id == row_id, g00, 0.0), axis=0, keepdims=True)
        d1 = jnp.sum(jnp.where(col_id == row_id, g11, 0.0), axis=0, keepdims=True)
        pack_lines(dbuf.at[e], d0, d1)
        for o in range(1, group):
            send(("d", e), dg(e, o))

    def pack_lines(ref, a, b):
        n = half // LANES
        for i in range(n):
            ref[i:i + 1, :] = a[:, i * LANES:(i + 1) * LANES]
            ref[n + i:n + i + 1, :] = b[:, i * LANES:(i + 1) * LANES]

    def stage_q1(e):
        q1(e).wait_recv()
        qacc[e] = qbuf[e, my_rows, :] + qsib[e]
        for k in far_first:
            send(("q2", e), q2(e, k))

    def stage_g1(e):
        g1(e).wait_recv()
        acc[e] = gbuf[e, my_rows, :] + gsib[e]
        for k in far_first:
            send(("g2", e), g2(e, k))

    def stage_q2(e):
        own = qacc[e, own_rows, :]
        for k in range(1, chips):
            q2(e, k).wait_recv()
            own = own + qpeer[e, k - 1]
        qall[e, my_piece, :] = own.astype(jnp.bfloat16)
        spread("q3", qall, my_piece, q3s, q3r, e)

    def stage_g2(e):
        tot = dbuf[e]
        for o in range(1, group):
            dg(e, o).wait_recv()
            tot = tot + dpeer[e, o - 1]
        n = half // LANES
        l0 = jnp.concatenate([tot[i:i + 1, :] for i in range(n)], axis=1)
        l1 = jnp.concatenate([tot[n + i:n + i + 1, :] for i in range(n)], axis=1)
        col = lax.broadcasted_iota(jnp.int32, (piece, half), 1)
        row = lax.broadcasted_iota(jnp.int32, (piece, half), 0) + first_row
        on = col == row
        up = col >= row
        c0 = jnp.sum(jnp.where(on, l0, 0.0), axis=1, keepdims=True)
        c1 = jnp.sum(jnp.where(on, l1, 0.0), axis=1, keepdims=True)
        diag_t = jnp.where(up, c0 + l0, c1 + l1)
        diag_o = c0 + l1
        own = acc[e, own_rows, :]
        for k in near_first:
            g2(e, k).wait_recv()
            own = own + gpeer[e, k - 1]
        k_t = jnp.where(on, 1.0, jnp.exp(-jnp.maximum(diag_t - 2.0 * own[:, 0:half], 0.0) / bandwidth))
        k_o = jnp.exp(-jnp.maximum(diag_o - 2.0 * own[:, half:], 0.0) / bandwidth)
        kbuf[e, my_piece, 0:half] = k_t.astype(jnp.bfloat16)
        kbuf[e, my_piece, half:] = k_o.astype(jnp.bfloat16)
        spread("g3", kbuf, my_piece, g3s, g3r, e)
        low = col < row
        row0 = jnp.sum(jnp.where(up, k_t, 0.0) + k_o, axis=1, keepdims=True)
        row1 = jnp.sum(jnp.where(low, k_t, 0.0), axis=1, keepdims=True) + 1.0
        s0 = jnp.sum(jnp.where(col > row, k_t, 0.0) + jnp.where(on, row0, 0.0), axis=0, keepdims=True)
        s1 = jnp.sum(jnp.where(low, k_t, 0.0) + k_o + jnp.where(on, row1, 0.0), axis=0, keepdims=True)
        pack_lines(sbuf.at[e, me], s0, s1)
        spread("t3", sbuf, me, t3s, t3r, e)

    def stage_y(e, t0, t1):
        if t0 == 0:
            gathered(qall, False, q3s, q3r, e)
            pj = qall[e].astype(jnp.float32)
            proj[e, 0:half, :] = jnp.where(lane_low, pj, 0.0).astype(jnp.bfloat16)
            proj[e, half:, :] = jnp.where(lane_low, 0.0, pj).astype(jnp.bfloat16)
        for t in range(t0, t1):
            sl = pl.ds(t * TILE, TILE)
            th = theta[e, :, sl]
            low = jnp.dot(proj[e], factor2[:, sl], preferred_element_type=jnp.float32)
            yn[e][:, sl] = ((th - mean[e:e + 1, sl]) * prec[0:1, sl] + low + (2.0 / bandwidth) * th).astype(jnp.bfloat16)

    def unpack(e):
        gathered(kbuf, False, g3s, g3r, e)
        for key in ("g1", "q1", "g2", "q2", "g3", "q3", "d", "t3"):
            drain((key, e))
        kern_ref, sums_ref = kern[e], sums[e]
        t = kbuf[e, :, 0:half].astype(jnp.float32)
        tt = t.T
        kern_ref[0:half, 0:half] = jnp.where(col_id >= row_id, t, tt).astype(jnp.bfloat16)
        kern_ref[half:, half:] = jnp.where(col_id <= row_id, t, tt).astype(jnp.bfloat16)
        ko = kbuf[e, :, half:]
        kern_ref[0:half, half:] = ko
        kern_ref[half:, 0:half] = ko.astype(jnp.float32).T.astype(jnp.bfloat16)
        gathered(sbuf, True, t3s, t3r, e)
        tot = sbuf[e, 0]
        for o in range(1, group):
            tot = tot + sbuf[e, o]
        tot = (2.0 / bandwidth) * tot
        for q in range(num_part // LANES):
            sums_ref[q * LANES:(q + 1) * LANES, :] = jnp.broadcast_to(tot[q:q + 1, :], (LANES, LANES)).T

    def update(e, last, t0, t1):
        for t in range(t0, t1):
            sl = pl.ds(t * TILE, TILE)
            new = advance(theta[e, :, sl], kern[e], yn[e][:, sl], sums[e], step_size, num_part)
            theta[e, :, sl] = new
            if last:
                continue
            theta_bf[e, :, sl] = new.astype(jnp.bfloat16)
            xb = (new - mean[e:e + 1, sl]).astype(jnp.bfloat16)
            part = dot_nt(xb, factor2[:, sl])
            if t == 0:
                proj_part[e] = part
            else:
                proj_part[e] += part

    first_rows(0)
    pl.semaphore_wait(barrier, group - 1)
    send_q(0)
    gram_and_send(0)
    stage_q1(0)
    first_rows(1)
    send_q(1)
    stage_g1(0)
    gram_and_send(1)
    stage_q1(1)
    stage_q2(0)
    stage_g1(1)
    stage_q2(1)
    stage_g2(0)
    stage_y(0, 0, 4)
    stage_g2(1)
    stage_y(1, 0, 4)
    unpack(0)
    update(0, False, 0, 4)
    send_q(0)
    gram_and_send(0)
    stage_q1(0)
    unpack(1)
    stage_g1(0)
    update(1, False, 0, 4)
    send_q(1)
    stage_q2(0)
    gram_and_send(1)
    stage_q1(1)
    stage_g1(1)
    stage_q2(1)
    stage_g2(0)
    stage_y(0, 0, 4)
    stage_g2(1)
    stage_y(1, 0, 4)
    unpack(0)
    update(0, False, 0, 4)
    send_q(0)
    gram_and_send(0)
    stage_q1(0)
    unpack(1)
    stage_g1(0)
    update(1, False, 0, 4)
    send_q(1)
    stage_q2(0)
    gram_and_send(1)
    stage_q1(1)
    stage_g1(1)
    stage_q2(1)
    stage_g2(0)
    stage_y(0, 0, 4)
    stage_g2(1)
    stage_y(1, 0, 4)
    unpack(0)
    update(0, True, 0, 4)
    unpack(1)
    for key in list(pending):
        drain(key)


def final_kernel(step_size, theta, kern, sums, yn, out_hbm, done, store_sem):
    num_ens, num_part, loc_feat = theta.shape
    stores = []
    for e in range(num_ens - 1):
        stores.append(pltpu.make_async_copy(theta.at[e], out_hbm.at[e], store_sem.at[e]))
        stores[-1].start()
    e = num_ens - 1
    for t in range(loc_feat // TILE):
        sl = pl.ds(t * TILE, TILE)
        done[t] = advance(theta[e, :, sl], kern, yn[:, sl], sums, step_size, num_part)
        stores.append(pltpu.make_async_copy(done.at[t], out_hbm.at[e, :, sl], store_sem.at[e + t]))
        stores[-1].start()
    for st in stores:
        st.wait()


def solution(mesh):
    feat_count = mesh.shape["feat"]
    cores = 2
    chips = feat_count // cores
    data_spec = P("ens", None, "feat")
    mean_spec = P("ens", "feat")
    prec_spec = P(("ens", "feat"))
    factor_spec = P(("ens", "feat"), None)

    def local_steps(particles, target_mean, precision, low_factor):
        num_ens, num_part, loc_feat = particles.shape
        rank = low_factor.shape[1]
        half = num_part // 2
        core_rows = half // cores
        piece = core_rows // chips
        lines = num_part // LANES
        step_size = 0.25 * loc_feat * feat_count
        prec_row = precision.reshape(1, loc_feat)
        low_t = low_factor.T
        f32, bf16 = jnp.float32, jnp.bfloat16
        vmem = pl.BlockSpec(memory_space=pltpu.VMEM)
        hbm = pl.BlockSpec(memory_space=pltpu.HBM)
        dma = pltpu.SemaphoreType.DMA
        nsem = num_ens * chips

        def sems(count, pairs):
            return [dma((count,))] * (2 * pairs)

        theta, kern, sums, yn = pl.pallas_call(
            functools.partial(exchange_kernel, cores, chips),
            out_shape=(
                jax.ShapeDtypeStruct((num_ens, num_part, loc_feat), f32),
                jax.ShapeDtypeStruct((num_part, num_part), bf16),
                jax.ShapeDtypeStruct((num_part, LANES), f32),
                jax.ShapeDtypeStruct((num_part, loc_feat), bf16),
            ),
            in_specs=[hbm] * 4,
            out_specs=(vmem,) * 4,
            scratch_shapes=[
                pltpu.VMEM((num_ens, num_part, loc_feat), bf16),
                pltpu.VMEM((num_ens, loc_feat), f32),
                pltpu.VMEM((1, loc_feat), f32),
                pltpu.VMEM((rank, loc_feat), bf16),
                pltpu.VMEM((2 * rank, loc_feat), bf16),
                pltpu.VMEM((num_part, num_part), bf16),
                pltpu.VMEM((num_part, LANES), f32),
                pltpu.VMEM((num_part, loc_feat), bf16),
                pltpu.VMEM((num_ens, num_part, 2 * rank), bf16),
                pltpu.VMEM((num_ens, num_part, 2 * rank), f32),
                pltpu.VMEM((num_part, num_part), f32),
                pltpu.VMEM((num_ens, half, num_part), f32),
                pltpu.VMEM((num_ens, core_rows, num_part), f32),
                pltpu.VMEM((num_ens, core_rows, num_part), f32),
                pltpu.VMEM((num_ens, chips - 1, piece, num_part), f32),
                pltpu.VMEM((num_ens, half, num_part), bf16),
                pltpu.VMEM((num_ens, half, 2 * rank), f32),
                pltpu.VMEM((num_ens, core_rows, 2 * rank), f32),
                pltpu.VMEM((num_ens, core_rows, 2 * rank), f32),
                pltpu.VMEM((num_ens, chips - 1, piece, 2 * rank), f32),
                pltpu.VMEM((num_ens, half, 2 * rank), bf16),
                pltpu.VMEM((num_ens, lines, LANES), f32),
                pltpu.VMEM((num_ens, feat_count - 1, lines, LANES), f32),
                pltpu.VMEM((num_ens, feat_count, lines, LANES), f32),
                dma((num_ens * CHUNKS,)),
                dma((3,)),
                *sems(num_ens, 1), *sems(nsem, 1), *sems(2 * nsem, 1),
                *sems(num_ens, 1), *sems(nsem, 1), *sems(2 * nsem, 1),
                *sems(num_ens * feat_count, 1), *sems(2 * nsem, 1),
            ],
            compiler_params=pltpu.CompilerParams(
                collective_id=0, has_side_effects=True, vmem_limit_bytes=VMEM_LIMIT),
            name="exchange",
        )(particles, *[pltpu.with_memory_space_constraint(v, pltpu.HBM) for v in (target_mean, prec_row, low_t)])
        tiles = loc_feat // TILE
        return pl.pallas_call(
            functools.partial(final_kernel, step_size),
            out_shape=jax.ShapeDtypeStruct((num_ens, num_part, loc_feat), f32),
            in_specs=[vmem] * 4,
            out_specs=hbm,
            scratch_shapes=[pltpu.VMEM((tiles, num_part, TILE), f32), dma((num_ens - 1 + tiles,))],
            compiler_params=pltpu.CompilerParams(vmem_limit_bytes=FINAL_LIMIT),
            name="final_update",
        )(theta, kern, sums, yn)

    return jax.shard_map(local_steps, mesh=mesh, in_specs=(data_spec, mean_spec, prec_spec, factor_spec),
                         out_specs=data_spec, check_vma=False)
```

time: 467 us -> 71 us (0.15); the launches traced: 459 us -> 70.9 us
  local copies, waits for them, and re-layouts: 198 us -> 0 us
  blocking collectives: 97 us -> 0 us
  matrix products: 80.9 us -> 0 us
  Pallas kernels: 0 us -> 70.7 us
  waiting for transfers between devices: 67.8 us -> 0 us
  between operations: 13.3 us -> 0.19 us
    psum x3 -> x0, local copies, waits for them, and re-layouts: 181 us -> none  [local_steps(): project, gram_mat = lax.psum((proj_part, gram_part), 'feat')]
    psum x3 -> x0, blocking collectives: 97 us -> none  [local_steps(): project, gram_mat = lax.psum((proj_part, gram_part), 'feat')]
    dot_general x9 -> x0, matrix products: 80.9 us -> none  [the longest x3 38.6 us: local_steps(): jnp.einsum('enm,emd->end', kernel.astype(jnp.bfloat16), mixed, preferred_...]
    pallas_call x0 -> x2, Pallas kernels: none -> 70.7 us  [the longest x1 67.4 us: local_steps(): pl.pallas_call(functools.partial(exchange_kernel, cores, chips), out_shap...]
    psum x3 -> x0, waiting for transfers between devices: 67.7 us -> none  [local_steps(): project, gram_mat = lax.psum((proj_part, gram_part), 'feat')]
    gather x6 -> x0, local copies, waits for them, and re-layouts: 16.9 us -> none  [local_steps(): gram_diag = jnp.diagonal(gram_mat, axis1=1, axis2=2)]
  transfers between devices with their start and end apart: 3 -> 0, of which waited for: 3 -> 0; matrix products, arithmetic and copies ran while one was open for 3% -> 0% of each run, Pallas kernels for 0% -> 0%
where the time goes in v3:
time: 71 us; the launch traced here: 70.9 us
  Pallas kernels  70.7 us (100%)
    pallas_call x1, Pallas kernels, local_steps(): pl.pallas_call(functools.partial(exchange_kernel, cores, chips), out_shap...  67.4 us
    pallas_call x1, Pallas kernels, local_steps(): pl.pallas_call(functools.partial(final_kernel, step_size), out_shape=jax....  3.34 us

profile of v3, /device:TPU:113, one launch (start us, length us, event | category | flops | bytes accessed | tf_op | source)
XLA Modules:
  0.0 70.9 jit_solution(9829674123183126551)
XLA Ops:
  0.0 67.4 %exchange.1 = (f32[2,512,2048]{2,1,0:T(8,128)S(1)}, bf16[512,512]{1,0:T(8,128)(2,1)S(1)}, f32[512,128]{1,0:T(8,128)S(1)}, bf16[512,2048]{1,0:T(8,128)(2,1)S(1)}) custom-call(f32[2,512,2048]{2,1,0:T(8,128)} %part_hbm.1, f32[2,2048]{1,0:T(2,128)} %mean_hbm.1, f32[1,2048]{1,0:T(1,128)} %bitcast.3, bf16[64,2048]{1,0:T(8,128)(2,1)} %bitcast.2), custom_call_target="tpu_custom_call" | custom-call | tf_op jit(solution)/shard_map/exchange/pallas_call | solution.py:390
  67.4 3.3 %final_update.1 = f32[2,512,2048]{2,1,0:T(8,128)} custom-call(f32[2,512,2048]{2,1,0:T(8,128)S(1)} %get-tuple-element.9.theta, bf16[512,512]{1,0:T(8,128)(2,1)S(1)} %get-tuple-element.10.kern, f32[512,128]{1,0:T(8,128)S(1)} %get-tuple-element.11.sums, bf16[512,2048]{1,0:T(8,128)(2,1)S(1)} %get-tuple-element.12.yn), custom_call_target="tpu_custom_call" | custom-call | tf_op jit(solution)/shard_map/final_update/pallas_call | solution.py:436

commit v4 on v3

--- a/solution.py
+++ b/solution.py
@@ -297,8 +297,8 @@
     stage_g1(1)
     stage_q2(1)
     stage_g2(0)
+    stage_g2(1)
     stage_y(0, 0, 4)
-    stage_g2(1)
     stage_y(1, 0, 4)
     unpack(0)
     update(0, False, 0, 4)
@@ -306,8 +306,10 @@
     gram_and_send(0)
     stage_q1(0)
     unpack(1)
+    update(1, False, 0, 1)
     stage_g1(0)
-    update(1, False, 0, 4)
+    update(1, False, 1, 2)
+    update(1, False, 2, 4)
     send_q(1)
     stage_q2(0)
     gram_and_send(1)
@@ -315,8 +317,8 @@
     stage_g1(1)
     stage_q2(1)
     stage_g2(0)
+    stage_g2(1)
     stage_y(0, 0, 4)
-    stage_g2(1)
     stage_y(1, 0, 4)
     unpack(0)
     update(0, False, 0, 4)
@@ -324,8 +326,10 @@
     gram_and_send(0)
     stage_q1(0)
     unpack(1)
+    update(1, False, 0, 1)
     stage_g1(0)
-    update(1, False, 0, 4)
+    update(1, False, 1, 2)
+    update(1, False, 2, 4)
     send_q(1)
     stage_q2(0)
     gram_and_send(1)
@@ -333,8 +337,8 @@
     stage_g1(1)
     stage_q2(1)
     stage_g2(0)
+    stage_g2(1)
     stage_y(0, 0, 4)
-    stage_g2(1)
     stage_y(1, 0, 4)
     unpack(0)
     update(0, True, 0, 4)

time: 71 us -> 70.3 us (level)
  no operation moved by 1% of the time
where the time goes in v4:
time: 70.3 us
  Pallas kernels  70.1 us (100%)
    pallas_call x1, Pallas kernels, local_steps(): pl.pallas_call(functools.partial(exchange_kernel, cores, chips), out_shap...  66.7 us
    pallas_call x1, Pallas kernels, local_steps(): pl.pallas_call(functools.partial(final_kernel, step_size), out_shape=jax....  3.34 us

profile of v4, /device:TPU:113, one launch (start us, length us, event | category | flops | bytes accessed | tf_op | source)
XLA Modules:
  0.0 70.3 jit_solution(8646753289089921338)
XLA Ops:
  0.0 66.7 %exchange.1 = (f32[2,512,2048]{2,1,0:T(8,128)S(1)}, bf16[512,512]{1,0:T(8,128)(2,1)S(1)}, f32[512,128]{1,0:T(8,128)S(1)}, bf16[512,2048]{1,0:T(8,128)(2,1)S(1)}) custom-call(f32[2,512,2048]{2,1,0:T(8,128)} %part_hbm.1, f32[2,2048]{1,0:T(2,128)} %mean_hbm.1, f32[1,2048]{1,0:T(1,128)} %bitcast.3, bf16[64,2048]{1,0:T(8,128)(2,1)} %bitcast.2), custom_call_target="tpu_custom_call" | custom-call | tf_op jit(solution)/shard_map/exchange/pallas_call | solution.py:394
  66.7 3.3 %final_update.1 = f32[2,512,2048]{2,1,0:T(8,128)} custom-call(f32[2,512,2048]{2,1,0:T(8,128)S(1)} %get-tuple-element.9.theta, bf16[512,512]{1,0:T(8,128)(2,1)S(1)} %get-tuple-element.10.kern, f32[512,128]{1,0:T(8,128)S(1)} %get-tuple-element.11.sums, bf16[512,2048]{1,0:T(8,128)(2,1)S(1)} %get-tuple-element.12.yn), custom_call_target="tpu_custom_call" | custom-call | tf_op jit(solution)/shard_map/final_update/pallas_call | solution.py:440
